TPU v7x, 32 devices: a whole 2x2x4 slice. The times are simulated.
32 devices in a mesh: group: 2 (over y), ctx: 4 (over z), head: 4 (over x, core).
Axes of the slice: x: 2, y: 2, z: 4, core: 2. Of those that a mesh axis runs over, the one named last changes fastest.
Arguments:
- query_nope: bfloat16 [512, 8192], P(('group', 'ctx'), 'head'), parts along dimension 0, may hold values from -6 to 6
- query_rope: bfloat16 [512, 4096], P(('group', 'ctx'), 'head'), parts along dimension 0, may hold values from -16 to 16
- kv_latent: bfloat16 [512, 512], P(('group', 'ctx'), 'head'), parts along dimension 0, may hold values from -1300 to 1300
- key_rope: bfloat16 [512, 64], P(('group', 'ctx')), parts along dimension 0, may hold values from -16 to 16
- latent_gain: float32 [512], replicated, may hold values from 0.1 to 1.9
- w_key: bfloat16 [512, 8192], P(None, 'head'), may hold values from -0.25 to 0.25
- w_value: bfloat16 [512, 8192], P(None, 'head'), may hold values from -0.25 to 0.25
- block_order: int32 [16], P('group'), parts along dimension 0, may hold values from 0 to 7, as said below
Outputs:
- attention_out: bfloat16 [512, 8192], P(('group', 'ctx'), 'head'), parts along dimension 0
There are 2 independent parts, one for each index of `group`. A program takes and returns all parts, laid end to end along the dimension named above; an argument that names none is the same for every part. Nothing has to cross between parts.
Inputs may be any that keep to these rules, and one draw needn't show every extreme that they name: `block_order`: A permutation of 0 to 7. Entries 2 c and 2 c + 1, for each c < 4, add up to 7.
All inputs are finite; a program needn't handle non-finite values.
Results may differ from a plain program's by a relative error of at most 0.0081.
Values may be sent and summed in bfloat16 or wider, within the bound.
A program may use at most 64 MiB of HBM per device.

v0:
```python
from functools import partial
import math
import jax
import jax.numpy as jnp
from jax import lax
from jax.sharding import PartitionSpec as P

ROPE = 64
NOPE = 128
VALUE_DIM = 128
EPSILON = 1e-06
NEGATIVE = -1e30


def rope_angle(positions, width):
    half_width = width // 2
    frequency = jnp.exp(-jnp.log(10000.0) * jnp.arange(half_width, dtype=jnp.float32) / half_width)
    return positions.astype(jnp.float32)[:, None] * frequency[None, :]


def rotate_pairs(values, angle):
    half_width = values.shape[-1] // 2
    first_half = values[..., :half_width]
    second = values[..., half_width:]
    cosine = jnp.cos(angle)
    sine_part = jnp.sin(angle)
    return jnp.concatenate(
        [first_half * cosine - second * sine_part, second * cosine + first_half * sine_part], -1
    )


def block_positions(begin_row, row_count, table, block_rows):
    row_ids = begin_row + jnp.arange(row_count, dtype=jnp.int32)
    blocks = row_ids // block_rows
    slot_ids = jnp.arange(table.shape[0], dtype=jnp.int32)
    looked = jnp.sum(jnp.where(blocks[:, None] == slot_ids[None, :], table[None, :], 0), axis=1)
    return looked * block_rows + row_ids % block_rows


def block_length(row_count, shard_rows):
    best_rows = shard_rows
    for factor in range(1, row_count // shard_rows + 1):
        if row_count // shard_rows % factor == 0 and shard_rows * factor <= max(512, shard_rows):
            best_rows = shard_rows * factor
    return best_rows


def attend_block(
    carried,
    query_latent,
    query_rotated,
    query_place,
    key_latent,
    key_rotated,
    key_place,
    score_scale,
):
    running_max, running_total, summed = carried
    contract = (((1,), (1,)), ((), ()))
    scores = lax.dot_general(query_latent, key_latent, contract, preferred_element_type=jnp.float32)
    scores = (
        scores
        + lax.dot_general(query_rotated, key_rotated, contract, preferred_element_type=jnp.float32)
    ) * score_scale
    visible = key_place[None, :] <= query_place[:, None]
    scores = jnp.where(visible, scores, NEGATIVE)
    new_max = jnp.maximum(running_max, jnp.max(scores, axis=1))
    exps = jnp.where(visible, jnp.exp(scores - new_max[:, None]), 0.0)
    shrink = jnp.exp(running_max - new_max)
    running_total = running_total * shrink + jnp.sum(exps, axis=1)
    summed = summed * shrink[:, None] + jnp.dot(
        exps.astype(jnp.bfloat16), key_latent, preferred_element_type=jnp.float32
    )
    return (new_max, running_total, summed)


def per_device(
    query_nope, query_rope, kv_latent, key_rope, latent_gain, w_key, w_value, block_order
):
    tokens_here = query_nope.shape[0]
    heads_here = w_key.shape[1] // NOPE
    latent_width = w_key.shape[0]
    block_rows = tokens_here // 2
    score_scale = 1.0 / math.sqrt(NOPE + ROPE)
    first_row = lax.axis_index("ctx") * tokens_here
    query_place = block_positions(first_row, tokens_here, block_order, block_rows)
    query_angle = rope_angle(query_place, ROPE)
    query_rotated = rotate_pairs(
        query_rope.astype(jnp.float32).reshape(tokens_here, heads_here, ROPE),
        query_angle[:, None, :],
    )
    query_rotated = query_rotated.astype(jnp.bfloat16).reshape(tokens_here * heads_here, ROPE)
    absorbed = jnp.einsum(
        "thd,lhd->thl",
        query_nope.reshape(tokens_here, heads_here, NOPE),
        w_key.reshape(latent_width, heads_here, NOPE),
        preferred_element_type=jnp.float32,
    )
    absorbed = absorbed.astype(jnp.bfloat16).reshape(tokens_here * heads_here, latent_width)
    row_place = jnp.repeat(query_place, heads_here)
    groups = ((absorbed, query_rotated, row_place),)
    initial = tuple(
        (
            (
                jnp.full((member[0].shape[0],), NEGATIVE, jnp.float32),
                jnp.zeros((member[0].shape[0],), jnp.float32),
                jnp.zeros((member[0].shape[0], latent_width), jnp.float32),
            )
            for member in groups
        )
    )
    columns = kv_latent.shape[1]
    column_part = kv_latent.astype(jnp.float32)
    square = lax.psum(jnp.sum(column_part * column_part, axis=1), "head")
    gain_part = lax.dynamic_slice_in_dim(latent_gain, lax.axis_index("head") * columns, columns, 0)
    scaled = (
        column_part * lax.rsqrt(square / latent_width + EPSILON)[:, None] * gain_part[None, :]
    ).astype(jnp.bfloat16)
    normed = lax.all_gather(scaled, "head", axis=1, tiled=True)
    key_rotated = rotate_pairs(key_rope.astype(jnp.float32), query_angle).astype(jnp.bfloat16)
    key_latent = lax.all_gather(normed, "ctx", axis=0, tiled=True)
    make_key_rotated = lax.all_gather(key_rotated, "ctx", axis=0, tiled=True)
    row_count = key_latent.shape[0]
    length = block_length(row_count, tokens_here)
    block_count = row_count // length
    latent_blocks = key_latent.reshape(block_count, length, latent_width)
    rotated_blocks = make_key_rotated.reshape(block_count, length, ROPE)
    block_starts = length * jnp.arange(block_count, dtype=jnp.int32)

    def one_block(state_now, operands):
        latent_block, rotated_block, first_key = operands
        key_place = block_positions(first_key, length, block_order, block_rows)
        updated = []
        for member, member_state in zip(groups, state_now):
            advance = partial(
                attend_block,
                query_latent=member[0],
                query_rotated=member[1],
                query_place=member[2],
                key_latent=latent_block,
                key_rotated=rotated_block,
                key_place=key_place,
                score_scale=score_scale,
            )
            updated.append(advance(member_state))
        return (tuple(updated), None)

    result, unused = lax.scan(one_block, initial, (latent_blocks, rotated_blocks, block_starts))
    mixed = jnp.concatenate(
        [
            (member_state[2] / member_state[1][:, None]).astype(jnp.bfloat16)
            for member_state in result
        ],
        0,
    )
    mixed = mixed.reshape(tokens_here, heads_here, latent_width)
    output = jnp.einsum(
        "thl,lhe->the",
        mixed,
        w_value.reshape(latent_width, heads_here, VALUE_DIM),
        preferred_element_type=jnp.float32,
    )
    return output.astype(jnp.bfloat16).reshape(tokens_here, heads_here * VALUE_DIM)


def solution(mesh):
    return jax.shard_map(
        per_device,
        mesh=mesh,
        in_specs=(
            P(("group", "ctx"), "head"),
            P(("group", "ctx"), "head"),
            P(("group", "ctx"), "head"),
            P(("group", "ctx"), None),
            P(),
            P(None, "head"),
            P(None, "head"),
            P("group"),
        ),
        out_specs=P(("group", "ctx"), "head"),
        check_vma=False,
    )
```

profile of v0, /device:TPU:0, one launch (start us, length us, event | category | flops | bytes accessed | tf_op | source)
XLA Modules:
  0.0 54.3 jit_solution(1356977436039085521)
XLA Ops:
  0.0 0.0 copy-start
  0.0 0.9 %dynamic_slice.12 = f32[128]{0:T(128)S(1)} dynamic-slice(f32[512]{0:T(512)} %param.12, s32[]{:T(128)S(6)} %select_n.69), dynamic_slice_sizes={128} | dynamic-slice | bytes 1028 | tf_op jit(solution)/shard_map/dynamic_slice | solution.py:115
  0.9 0.8 %fusion.33 = f32[64]{0:T(128)S(1)} fusion(bf16[64,128]{1,0:T(8,128)(2,1)} %param.10), kind=kLoop, calls=%fused_computation.34 | loop fusion | flops 24512 | bytes 16640 | tf_op jit(solution)/shard_map/reduce_sum | solution.py:114
  1.7 8.4 %psum.7 = f32[64]{0:T(128)S(1)} all-reduce(f32[64]{0:T(128)S(1)} %fusion.33), channel_id=1, replica_groups=mesh['group'=2,'ctx'=4,'head'=4] {'head'}, use_global_device_ids=true, to_apply=%region_3.4 | all-reduce | flops 64 | bytes 512 | tf_op jit(solution)/shard_map/psum | solution.py:114
  10.1 0.8 %fusion.35 = bf16[64,128]{1,0:T(8,128)(2,1)S(1)} fusion(bf16[64,128]{1,0:T(8,128)(2,1)} %param.10, f32[128]{0:T(128)S(1)} %dynamic_slice.12, f32[64]{0:T(128)S(1)} %add_rsqrt_fusion), kind=kLoop, calls=%fused_computation.36 | loop fusion | flops 32768 | bytes 33536 | tf_op jit(solution)/shard_map/convert_element_type | solution.py:118
  10.9 5.3 %all_gather.9 = bf16[64,512]{1,0:T(8,128)(2,1)S(1)} all-gather(bf16[64,128]{1,0:T(8,128)(2,1)S(1)} %fusion.35), channel_id=1, replica_groups=mesh['group'=2,'ctx'=4,'head'=4] {'head'}, dimensions={1}, use_global_device_ids=true | all-gather | bytes 81920 | tf_op jit(solution)/shard_map/all_gather | solution.py:119
  16.2 14.1 %all_gather.10 = bf16[256,512]{1,0:T(8,128)(2,1)S(1)} all-gather(bf16[64,512]{1,0:T(8,128)(2,1)S(1)} %all_gather.9), channel_id=1, replica_groups=mesh['group'=2,'ctx'=4,'head'=4] {'ctx'}, dimensions={0}, use_global_device_ids=true | all-gather | bytes 327680 | tf_op jit(solution)/shard_map/all_gather | solution.py:121
  30.2 0.0 copy-done
  30.2 1.8 %fusion.9 = bf16[64,16,512]{2,0,1:T(8,128)(2,1)S(1)} fusion(bf16[512,2048]{1,0:T(8,128)(2,1)S(1)} %copy-done, bf16[64,2048]{1,0:T(8,128)(2,1)} %param.8), kind=kOutput, calls=%fused_computation.8 | convolution fusion | flops 134742016 | bytes 3407872 | tf_op jit(solution)/shard_map/thd,lhd->thl/dot_general | solution.py:93
  32.0 0.0 copy-start.3
  32.1 0.0 copy-start.2
  32.1 0.0 copy-start.1
  32.1 0.6 %copy.21 = bf16[64,16,512]{2,1,0:T(8,128)(2,1)S(1)} copy(bf16[64,16,512]{2,0,1:T(8,128)(2,1)S(1)} %fusion.9) | data formatting | bytes 2097152 | tf_op jit(solution)/shard_map/convert_element_type | solution.py:99
  32.7 1.5 %fusion.46 = f32[1024,256]{0,1:T(8,128)} fusion(bf16[1024,512]{1,0:T(8,128)(2,1)S(1)} %bitcast.45, bf16[256,512]{1,0:T(8,128)(2,1)S(1)} %all_gather.10), kind=kOutput, calls=%fused_computation.68 | convolution fusion | flops 268435456 | bytes 2359296 | tf_op jit(solution)/shard_map/while/body/eval_jaxpr/dot_general | solution.py:60
  34.1 0.0 copy-done.3
  34.2 0.1 select_reduce_fusion.1
  34.3 0.0 copy-done.2
  34.3 0.2 multiply_cosine_fusion
  34.5 0.1 pad_maximum_fusion
  34.6 13.3 %all_gather.11 = bf16[256,64]{1,0:T(8,128)(2,1)S(1)} all-gather(bf16[64,64]{1,0:T(8,128)(2,1)S(1)} %pad_maximum_fusion), channel_id=1, replica_groups=mesh['group'=2,'ctx'=4,'head'=4] {'ctx'}, dimensions={0}, use_global_device_ids=true | all-gather | bytes 40960 | tf_op jit(solution)/shard_map/all_gather | solution.py:122
  47.9 0.0 copy-done.1
  47.9 0.1 reshape.178
  48.0 0.2 subtract_convert_fusion
  48.2 0.1 broadcast_in_dim.74
  48.3 0.1 le.23
  48.4 0.1 select_reduce_fusion
  48.5 1.7 %fusion.45 = (f32[1024]{0:T(1024)S(1)}, f32[1024,256]{0,1:T(8,128)S(1)}) fusion(f32[1024,256]{0,1:T(8,128)} %fusion.46, bf16[256,64]{1,0:T(8,128)(2,1)S(1)} %all_gather.11, bf16[1024,32]{1,0:T(8,128)(2,1)S(1)} %bitcast.47, bf16[1024,32]{1,0:T(8,128)(2,1)S(1)} %bitcast.46, s32[1024]{0:T(1024)S(1)} %le.23, s32[256]{0:T(256)S(1)} %fusion.38), kind=kOutput, calls=%fused_computation.67 | convolution fusion | flops 35126272 | bytes 2270208 | tf_op jit(solution)/shard_map/while/body/eval_jaxpr/dot_general | solution.py:63
  50.2 0.2 fusion.21
  50.4 0.0 copy-start.4
  50.4 0.6 %divide_convert_fusion = bf16[1024,512]{1,0:T(8,128)(2,1)S(1)} fusion(bf16[256,512]{1,0:T(8,128)(2,1)S(1)} %all_gather.10, f32[1024]{0:T(1024)S(1)} %get-tuple-element.40, f32[1024]{0:T(1024)S(1)} %get-tuple-element.29, f32[1024,256]{0,1:T(8,128)S(1)} %get-tuple-element.48, f32[1024]{0:T(1024)S(1)} %broadcast_maximum_fusion, s32[1024]{0:T(1024)S(1)} %le.23, ...), kind=kOutput, calls=%fused_computation.6 | convolution fusion | flops 271056896 | bytes 2376704 | tf_op jit(solution)/shard_map/while/body/eval_jaxpr/dot_general | solution.py:71
  51.0 1.0 %copy-done.4 = bf16[512,2048]{1,0:T(8,128)(2,1)S(1)} copy-done((bf16[512,2048]{1,0:T(8,128)(2,1)S(1)}, bf16[512,2048]{1,0:T(8,128)(2,1)}, u32[]{:S(2)}) %copy-start.4) | copy-done | bytes 2097176
  52.0 1.5 %fusion.17 = bf16[16,8,8,128]{3,2,1,0:T(8,128)(2,1)S(1)} fusion(bf16[64,16,512]{2,1,0:T(8,128)(2,1)S(1)} %bitcast.48, bf16[512,2048]{1,0:T(8,128)(2,1)S(1)} %copy-done.4), kind=kOutput, calls=%fused_computation.14 | convolution fusion | flops 134348800 | bytes 3407872 | tf_op jit(solution)/shard_map/thl,lhe->the/dot_general | solution.py:157
  53.5 0.8 %copy.52 = bf16[16,8,8,128]{3,2,0,1:T(8,128)(2,1)} copy(bf16[16,8,8,128]{3,2,1,0:T(8,128)(2,1)S(1)} %fusion.17) | data formatting | bytes 524288 | tf_op jit(solution)/shard_map/reshape | solution.py:163
  (9 shorter events, 0.1 us)
Async XLA Ops:
  0.0 30.2 %copy-start = (bf16[512,2048]{1,0:T(8,128)(2,1)S(1)}, bf16[512,2048]{1,0:T(8,128)(2,1)}, u32[]{:S(2)}) copy-start(bf16[512,2048]{1,0:T(8,128)(2,1)} %param.13) | copy-start | bytes 6291460
  32.0 2.1 %copy-start.3 = (s32[8]{0:T(128)S(1)}, s32[8]{0:T(128)}, u32[]{:S(2)}) copy-start(s32[8]{0:T(128)} %param.15) | copy-start | bytes 100
  32.1 2.2 %copy-start.2 = (bf16[64,64]{1,0:T(8,128)(2,1)S(1)}, bf16[64,64]{1,0:T(8,128)(2,1)}, u32[]{:S(2)}) copy-start(bf16[64,64]{1,0:T(8,128)(2,1)} %param.11) | copy-start | bytes 24580
  32.1 15.8 %copy-start.1 = (bf16[64,1024]{1,0:T(8,128)(2,1)S(1)}, bf16[64,1024]{1,0:T(8,128)(2,1)}, u32[]{:S(2)}) copy-start(bf16[64,1024]{1,0:T(8,128)(2,1)} %param.9) | copy-start | bytes 393220
  50.4 1.6 %copy-start.4 = (bf16[512,2048]{1,0:T(8,128)(2,1)S(1)}, bf16[512,2048]{1,0:T(8,128)(2,1)}, u32[]{:S(2)}) copy-start(bf16[512,2048]{1,0:T(8,128)(2,1)} %param.14) | copy-start | bytes 6291460
where the time goes:
time: 54.7 us; the launch traced here: 54.3 us
  blocking collectives  41 us (75%)
  matrix products  7 us (13%)
  local copies, waits for them, and re-layouts  3.53 us (6%)
  other arithmetic  2.6 us (5%)
    all_gather x1, blocking collectives, per_device(): key_latent = lax.all_gather(normed, 'ctx', axis=0, tiled=True)  14.1 us
    all_gather x1, blocking collectives, per_device(): make_key_rotated = lax.all_gather(key_rotated, 'ctx', axis=0, tiled=True)  13.3 us
    psum x1, blocking collectives, per_device(): square = lax.psum(jnp.sum(column_part * column_part, axis=1), 'head')  8.37 us
    all_gather x1, blocking collectives, per_device(): normed = lax.all_gather(scaled, 'head', axis=1, tiled=True)  5.25 us
    dot_general x1, matrix products, per_device(): jnp.einsum('thd,lhd->thl', query_nope.reshape(tokens_here, heads_here, NO...  1.79 us
    dot_general x1, matrix products, attend_block(): lax.dot_general(query_rotated, key_rotated, contract, preferred_element_t...  1.65 us
    dot_general x1, matrix products, per_device(): jnp.einsum('thl,lhe->the', mixed, w_value.reshape(latent_width, heads_her...  1.49 us
    dot_general x1, matrix products, attend_block(): lax.dot_general(query_latent, key_latent, contract, preferred_element_typ...  1.46 us

commit v1 on v0

--- a/solution.py
+++ b/solution.py
@@ -118,8 +118,11 @@
     ).astype(jnp.bfloat16)
     normed = lax.all_gather(scaled, "head", axis=1, tiled=True)
     key_rotated = rotate_pairs(key_rope.astype(jnp.float32), query_angle).astype(jnp.bfloat16)
-    key_latent = lax.all_gather(normed, "ctx", axis=0, tiled=True)
-    make_key_rotated = lax.all_gather(key_rotated, "ctx", axis=0, tiled=True)
+    key_latent, make_key_rotated = jnp.split(
+        lax.all_gather(jnp.concatenate([normed, key_rotated], axis=1), "ctx", axis=0, tiled=True),
+        [normed.shape[1]],
+        axis=1,
+    )
     row_count = key_latent.shape[0]
     length = block_length(row_count, tokens_here)
     block_count = row_count // length

time: 54.7 us -> 43.2 us (0.79)
  blocking collectives: 41 us -> 28.1 us
  other arithmetic: 2.6 us -> 3.98 us
    all_gather x2 -> x1, blocking collectives: 27.4 us -> 14.5 us  [per_device(): lax.all_gather(jnp.concatenate([normed, key_rotated], axis=1), 'ctx', axi...]
    convert_element_type x1, other arithmetic: 0.01 us -> 0.72 us  [per_device(): key_rope.astype(jnp.float32)]
    reduce_sum x2, other arithmetic: 0.17 us -> 0.82 us  [block_positions(): jnp.sum(jnp.where(blocks[:, None] == slot_ids[None, :], table[None, :], 0...]
where the time goes in v1:
time: 43.2 us; the launch traced here: 42.7 us
  blocking collectives  28.1 us (65%)
  matrix products  7.02 us (16%)
  other arithmetic  3.98 us (9%)
  local copies, waits for them, and re-layouts  3.51 us (8%)
    all_gather x1, blocking collectives, per_device(): lax.all_gather(jnp.concatenate([normed, key_rotated], axis=1), 'ctx', axi...  14.5 us
    psum x1, blocking collectives, per_device(): square = lax.psum(jnp.sum(column_part * column_part, axis=1), 'head')  8.37 us
    all_gather x1, blocking collectives, per_device(): normed = lax.all_gather(scaled, 'head', axis=1, tiled=True)  5.25 us
    dot_general x1, matrix products, per_device(): jnp.einsum('thd,lhd->thl', query_nope.reshape(tokens_here, heads_here, NO...  1.79 us
    dot_general x1, matrix products, attend_block(): lax.dot_general(query_rotated, key_rotated, contract, preferred_element_t...  1.65 us
    dot_general x1, matrix products, per_device(): jnp.einsum('thl,lhe->the', mixed, w_value.reshape(latent_width, heads_her...  1.49 us
    dot_general x1, matrix products, attend_block(): lax.dot_general(query_latent, key_latent, contract, preferred_element_typ...  1.46 us
    unnamed x8, local copies, waits for them, and re-layouts  0.97 us

profile of v1, /device:TPU:0, one launch (start us, length us, event | category | flops | bytes accessed | tf_op | source)
XLA Modules:
  0.0 42.7 jit_solution(16274263337563931323)
XLA Ops:
  0.0 0.0 copy-start
  0.0 0.9 %dynamic_slice.12 = f32[128]{0:T(128)S(1)} dynamic-slice(f32[512]{0:T(512)} %param.12, s32[]{:T(128)S(6)} %select_n.69), dynamic_slice_sizes={128} | dynamic-slice | bytes 1028 | tf_op jit(solution)/shard_map/dynamic_slice | solution.py:115
  0.9 0.8 %fusion.37 = f32[64]{0:T(128)S(1)} fusion(bf16[64,128]{1,0:T(8,128)(2,1)} %param.10), kind=kLoop, calls=%fused_computation.39 | loop fusion | flops 24512 | bytes 16640 | tf_op jit(solution)/shard_map/reduce_sum | solution.py:114
  1.7 8.4 %psum.7 = f32[64]{0:T(128)S(1)} all-reduce(f32[64]{0:T(128)S(1)} %fusion.37), channel_id=1, replica_groups=mesh['group'=2,'ctx'=4,'head'=4] {'head'}, use_global_device_ids=true, to_apply=%region_3.4 | all-reduce | flops 64 | bytes 512 | tf_op jit(solution)/shard_map/psum | solution.py:114
  10.1 0.8 %fusion.39 = bf16[64,128]{1,0:T(8,128)(2,1)S(1)} fusion(bf16[64,128]{1,0:T(8,128)(2,1)} %param.10, f32[128]{0:T(128)S(1)} %dynamic_slice.12, f32[64]{0:T(128)S(1)} %add_rsqrt_fusion), kind=kLoop, calls=%fused_computation.41 | loop fusion | flops 32768 | bytes 33536 | tf_op jit(solution)/shard_map/convert_element_type | solution.py:118
  10.9 5.3 %all_gather.6 = bf16[64,512]{1,0:T(8,128)(2,1)S(1)} all-gather(bf16[64,128]{1,0:T(8,128)(2,1)S(1)} %fusion.39), channel_id=1, replica_groups=mesh['group'=2,'ctx'=4,'head'=4] {'head'}, dimensions={1}, use_global_device_ids=true | all-gather | bytes 81920 | tf_op jit(solution)/shard_map/all_gather | solution.py:119
  16.2 0.7 %select_reduce_fusion.1 = s32[64]{0:T(128)S(1)} fusion(s32[8]{0:T(128)} %param.15, s32[64]{0:T(128)S(1)} %and_select_fusion.1), kind=kLoop, calls=%fused_computation.47 | loop fusion | flops 1472 | bytes 544 | tf_op jit(solution)/shard_map/reduce_sum | solution.py:36
  16.9 0.7 %convert_element_type.43 = f32[64,64]{1,0:T(8,128)S(1)} convert(bf16[64,64]{1,0:T(8,128)(2,1)} %param.11) | non-fusion elementwise | flops 4096 | bytes 24576 | tf_op jit(solution)/shard_map/convert_element_type | solution.py:120
  17.7 0.2 multiply_cosine_fusion
  17.9 0.1 pad_maximum_fusion
  17.9 14.5 %all_gather.7 = bf16[256,576]{1,0:T(8,128)(2,1)S(1)} all-gather(bf16[64,576]{1,0:T(8,128)(2,1)S(1)} %pad_maximum_fusion), channel_id=1, replica_groups=mesh['group'=2,'ctx'=4,'head'=4] {'ctx'}, dimensions={0}, use_global_device_ids=true | all-gather | bytes 368640 | tf_op jit(solution)/shard_map/all_gather | solution.py:122
  32.4 0.0 copy-done
  32.4 1.8 %fusion.9 = bf16[64,16,512]{2,0,1:T(8,128)(2,1)S(1)} fusion(bf16[512,2048]{1,0:T(8,128)(2,1)S(1)} %copy-done, bf16[64,2048]{1,0:T(8,128)(2,1)} %param.8), kind=kOutput, calls=%fused_computation.8 | convolution fusion | flops 134742016 | bytes 3407872 | tf_op jit(solution)/shard_map/thd,lhd->thl/dot_general | solution.py:93
  34.2 0.0 copy-start.1
  34.2 0.6 %copy.21 = bf16[64,16,512]{2,1,0:T(8,128)(2,1)S(1)} copy(bf16[64,16,512]{2,0,1:T(8,128)(2,1)S(1)} %fusion.9) | data formatting | bytes 2097152 | tf_op jit(solution)/shard_map/convert_element_type | solution.py:99
  34.8 0.0 copy-start.2
  34.8 1.5 %fusion.34 = f32[1024,256]{0,1:T(8,128)} fusion(bf16[1024,512]{1,0:T(8,128)(2,1)S(1)} %bitcast.42, bf16[256,576]{1,0:T(8,128)(2,1)S(1)} %all_gather.7), kind=kOutput, calls=%fused_computation.31 | convolution fusion | flops 268435456 | bytes 2359296 | tf_op jit(solution)/shard_map/while/body/eval_jaxpr/dot_general | solution.py:60
  36.3 0.0 copy-done.1
  36.3 0.1 reshape.178
  36.5 0.2 subtract_convert_fusion
  36.7 0.1 broadcast_in_dim.74
  36.8 0.1 le.23
  36.8 0.0 copy-done.2
  36.9 0.1 select_reduce_fusion
  36.9 1.6 %fusion.49 = (f32[1024]{0:T(1024)S(1)}, f32[1024,256]{0,1:T(8,128)S(1)}) fusion(f32[1024,256]{0,1:T(8,128)} %fusion.34, bf16[256,576]{1,0:T(8,128)(2,1)S(1)} %all_gather.7, bf16[1024,32]{1,0:T(8,128)(2,1)S(1)} %bitcast.44, bf16[1024,32]{1,0:T(8,128)(2,1)S(1)} %bitcast.43, s32[1024]{0:T(1024)S(1)} %le.23, s32[256]{0:T(256)S(1)} %fusion.42), kind=kOutput, calls=%fused_computation.71 | convolution fusion | flops 35126272 | bytes 2696192 | tf_op jit(solution)/shard_map/while/body/eval_jaxpr/dot_general | solution.py:63
  38.6 0.2 fusion.21
  38.9 0.0 copy-start.3
  38.9 0.6 %divide_convert_fusion = bf16[1024,512]{1,0:T(8,128)(2,1)S(1)} fusion(f32[1024]{0:T(1024)S(1)} %get-tuple-element.40, f32[1024]{0:T(1024)S(1)} %get-tuple-element.29, f32[1024,256]{0,1:T(8,128)S(1)} %get-tuple-element.48, f32[1024]{0:T(1024)S(1)} %broadcast_maximum_fusion, s32[1024]{0:T(1024)S(1)} %le.23, s32[256]{0:T(256)S(1)} %fusion.42, ...), kind=kOutput, calls=%fused_computation.6 | convolution fusion | flops 271056896 | bytes 2376704 | tf_op jit(solution)/shard_map/while/body/eval_jaxpr/dot_general | solution.py:71
  39.5 1.0 %copy-done.3 = bf16[512,2048]{1,0:T(8,128)(2,1)S(1)} copy-done((bf16[512,2048]{1,0:T(8,128)(2,1)S(1)}, bf16[512,2048]{1,0:T(8,128)(2,1)}, u32[]{:S(2)}) %copy-start.3) | copy-done | bytes 2097176
  40.5 1.5 %fusion.17 = bf16[16,8,8,128]{3,2,1,0:T(8,128)(2,1)S(1)} fusion(bf16[64,16,512]{2,1,0:T(8,128)(2,1)S(1)} %bitcast.45, bf16[512,2048]{1,0:T(8,128)(2,1)S(1)} %copy-done.3), kind=kOutput, calls=%fused_computation.14 | convolution fusion | flops 134348800 | bytes 3407872 | tf_op jit(solution)/shard_map/thl,lhe->the/dot_general | solution.py:160
  42.0 0.8 %copy.52 = bf16[16,8,8,128]{3,2,0,1:T(8,128)(2,1)} copy(bf16[16,8,8,128]{3,2,1,0:T(8,128)(2,1)S(1)} %fusion.17) | data formatting | bytes 524288 | tf_op jit(solution)/shard_map/reshape | solution.py:166
  (8 shorter events, 0.1 us)
Async XLA Ops:
  0.0 32.4 %copy-start = (bf16[512,2048]{1,0:T(8,128)(2,1)S(1)}, bf16[512,2048]{1,0:T(8,128)(2,1)}, u32[]{:S(2)}) copy-start(bf16[512,2048]{1,0:T(8,128)(2,1)} %param.13) | copy-start | bytes 6291460
  34.2 2.1 %copy-start.1 = (bf16[64,1024]{1,0:T(8,128)(2,1)S(1)}, bf16[64,1024]{1,0:T(8,128)(2,1)}, u32[]{:S(2)}) copy-start(bf16[64,1024]{1,0:T(8,128)(2,1)} %param.9) | copy-start | bytes 393220
  34.8 2.0 %copy-start.2 = (s32[8]{0:T(128)S(1)}, s32[8]{0:T(128)}, u32[]{:S(2)}) copy-start(s32[8]{0:T(128)} %param.15) | copy-start | bytes 100
  38.9 1.6 %copy-start.3 = (bf16[512,2048]{1,0:T(8,128)(2,1)S(1)}, bf16[512,2048]{1,0:T(8,128)(2,1)}, u32[]{:S(2)}) copy-start(bf16[512,2048]{1,0:T(8,128)(2,1)} %param.14) | copy-start | bytes 6291460
